TPU v7x, 128 devices: a whole 4x4x4 slice. The times are simulated.
128 devices in a mesh: row: 4 (over z_lo, core), col: 32 (over z_hi, y, x).
Axes of the slice: x: 4, y: 4, z: 4 (z_hi: 2, z_lo: 2; z = z_hi * 2 + z_lo), core: 2. Of those that a mesh axis runs over, the one named last changes fastest.
Arguments:
- source_terms: float32 [256, 2048, 256], P('row', 'col'), may hold values from -6 to 6
- initial_values: float32 [256, 2048, 256], P('row', 'col'), may hold values from -6 to 6
- absorption: float32 [256, 2048, 256], P('row', 'col'), may hold values from 0.1 to 0.9
Outputs:
- improved: float32 [256, 2048, 256], P('row', 'col')
- remaining: float32 [256, 2048, 256], P('row', 'col')
All inputs are finite; a program needn't handle non-finite values.
Results may differ from a plain program's by a relative error of at most 0.000043.
Values sent between devices are 32-bit elements; how exact they have to be, the bound alone decides.
A program may use at most 128 MiB of HBM per device.

v0:
```python
import functools

import jax
import jax.numpy as jnp
from jax import lax
from jax.experimental import pallas as pl
from jax.experimental.pallas import tpu as pltpu
from jax.sharding import PartitionSpec as P

RATIO = 4
INNER = 9
LANES = 128
ROW_PAD = 4
COL_PAD = 8
DEEP = INNER
COARSE_PAD = 16
MESH = pl.DeviceIdType.MESH


def edge_rects(rows, cols, near, far):
    (y0, ny), (x0, nx) = rows, cols
    wide = far - near
    return [
        (0, 1, (y0, ny, x0 + nx - far, wide), (y0, ny, x0 - far, wide)),
        (0, -1, (y0, ny, x0 + near, wide), (y0, ny, x0 + nx + near, wide)),
        (1, 0, (y0 + ny - far, wide, x0, nx), (y0 - far, wide, x0, nx)),
        (-1, 0, (y0 + near, wide, x0, nx), (y0 + ny + near, wide, x0, nx)),
    ]


def corner_rects(rows, cols, near_y, far_y, far_x):
    (y0, ny), (x0, nx) = rows, cols
    wide = far_y - near_y
    found = []
    for dy in (1, -1):
        if dy == 1:
            from_y, to_y = y0 + ny - far_y, y0 - far_y
        else:
            from_y, to_y = y0 + near_y, y0 + ny + near_y
        for dx in (1, -1):
            if dx == 1:
                from_x, to_x = x0 + nx - far_x, x0 - far_x
            else:
                from_x, to_x = x0, x0 + nx
            found.append((dy, dx, (from_y, wide, from_x, far_x), (to_y, wide, to_x, far_x)))
    return found


def plan(ny, nx):
    rows, cols = (ROW_PAD, ny), (COL_PAD, nx)
    crows, ccols = (DEEP, ny // RATIO), (COARSE_PAD, nx // RATIO)
    coarse = edge_rects(crows, ccols, 0, DEEP)
    for step in range(3):
        coarse = coarse + corner_rects(crows, ccols, 3 * step, 3 * step + 3, DEEP - 3 * step)
    exchanges = {
        "u0": edge_rects(rows, cols, 0, 1),
        "f": edge_rects(rows, cols, 0, 2) + corner_rects(rows, cols, 0, 2, 2),
        "r": edge_rects(rows, cols, 0, 2) + corner_rects(rows, cols, 0, 2, 2),
        "u1": edge_rects(rows, cols, 0, 3) + corner_rects(rows, cols, 0, 2, 2),
        "cr": coarse,
        "f3": edge_rects(rows, cols, 2, 3),
        "r3": edge_rects(rows, cols, 2, 3),
        "cl": coarse,
        "u3": edge_rects(rows, cols, 0, 4) + corner_rects(rows, cols, 0, 3, 3),
    }
    at, first = 0, {}
    for name, rects in exchanges.items():
        first[name] = at
        at += len(rects)
    return exchanges, first, at


def kernel(sizes, f_hbm, u_hbm, a_hbm, improved_hbm, remaining_hbm,
           ua, ub, uc, ud, f, r, d, sums, spread, cl, cr, ca, cb,
           load_sem, store_sem, send_sem, recv_sem):
    ny, nx, halves, n_row, n_col = sizes
    cy, cx = ny // RATIO, nx // RATIO
    exchanges, first, _ = plan(ny, nx)
    me_row, me_col = lax.axis_index("row"), lax.axis_index("col")

    def neighbour(dy, dx):
        return (lax.rem(me_row + dy + n_row, n_row), lax.rem(me_col + dx + n_col, n_col))

    def box(ref, where):
        y, h, x, w = where
        return ref.at[pl.ds(y, h), :, pl.ds(x, w), :]

    def copies(name, source, landing):
        made = []
        for k, (dy, dx, src, dst) in enumerate(exchanges[name]):
            made.append(pltpu.make_async_remote_copy(
                src_ref=box(source, src), dst_ref=box(landing, dst),
                send_sem=send_sem.at[first[name] + k], recv_sem=recv_sem.at[first[name] + k],
                device_id=neighbour(dy, dx), device_id_type=MESH))
        return made

    sent = []

    def send(name, source, landing):
        made = copies(name, source, landing)
        for copy in made:
            copy.start()
        sent.append((name, made))
        return made

    def arrived(made):
        for copy in made:
            copy.wait_recv()

    def loads(k, hbm, ref, y0, x0):
        made = []
        for h in range(halves):
            made.append(pltpu.make_async_copy(
                hbm.at[:, :, pl.ds(h * LANES, LANES)],
                ref.at[pl.ds(y0, ny), h, pl.ds(x0, nx), :],
                load_sem.at[k * halves + h]))
        for copy in made:
            copy.start()
        return made

    a_loads = loads(0, a_hbm, d, 0, 0)
    u_loads = loads(1, u_hbm, ua, ROW_PAD, COL_PAD)
    f_loads = loads(2, f_hbm, f, ROW_PAD, COL_PAD)

    barrier = pltpu.get_barrier_semaphore()
    around = [(dy, dx) for dy in (-1, 0, 1) for dx in (-1, 0, 1) if (dy, dx) != (0, 0)]
    for dy, dx in around:
        pl.semaphore_signal(barrier, inc=1, device_id=neighbour(dy, dx), device_id_type=MESH)

    own = [COL_PAD + 8 * k for k in range(nx // 8)]

    def windows(x0, n, reach):
        low, high = x0 - reach, x0 + n + reach
        return [min(x, high - 8) for x in range(low, high, 8)]

    def at(ref, y, h, x):
        return ref[y, h, pl.ds(x, 8), :]

    def coarse_sums(ref, done):
        def body(y, carry):
            for h in range(halves):
                for g in range(cx // 8):
                    parts = [sums[y, h, pl.ds(32 * g + k, 8, stride=4), :] for k in range(4)]
                    total = ((parts[0] + parts[1]) + (parts[2] + parts[3])) * 0.25
                    done(y, h, g, total)
            return carry
        lax.fori_loop(0, cy, body, 0)

    for copy in a_loads:
        copy.wait()

    def prepare(y, carry):
        for h in range(halves):
            for k in range(nx // 8):
                total = None
                for j in range(RATIO):
                    a = d[RATIO * y + j, h, pl.ds(8 * k, 8), :]
                    here = 4.0 + a
                    d[RATIO * y + j, h, pl.ds(8 * k, 8), :] = here
                    r[ROW_PAD + RATIO * y + j, h, pl.ds(COL_PAD + 8 * k, 8), :] = 0.8 / here
                    total = a if total is None else total + a
                sums[y, h, pl.ds(8 * k, 8), :] = total
        return carry
    lax.fori_loop(0, cy, prepare, 0)

    def keep_mass(y, h, g, total):
        cr[DEEP + y, h, pl.ds(COARSE_PAD + 8 * g, 8), :] = 0.8 / (4.0 + total)
    coarse_sums(sums, keep_mass)

    pl.semaphore_wait(barrier, len(around))
    for copy in u_loads:
        copy.wait()
    u0 = send("u0", ua, ua)
    for copy in f_loads:
        copy.wait()
    f2 = send("f", f, f)
    r2 = send("r", r, r)

    def sweep(src, dst, reach, starts, load, rate, top, count, step=2):
        def body(i, carry):
            y = top - reach + step * i
            for h in range(halves):
                for x in starts:
                    column = [at(src, y + j, h, x) for j in range(-1, step + 1)]
                    for j in range(step):
                        total = (column[j] + column[j + 2]) + (at(src, y + j, h, x - 1) + at(src, y + j, h, x + 1))
                        new = 0.2 * column[j + 1] + at(rate, y + j, h, x) * (at(load, y + j, h, x) + total)
                        dst[y + j, h, pl.ds(x, 8), :] = new
            return carry
        lax.fori_loop(0, (count + 2 * reach) // step, body, 0)

    def left_over(src, y, h, x):
        column = [at(src, y + j, h, x) for j in range(-1, RATIO + 1)]
        found = []
        for j in range(RATIO):
            total = (column[j] + column[j + 2]) + (at(src, y + j, h, x - 1) + at(src, y + j, h, x + 1))
            here = d[y + j - ROW_PAD, h, pl.ds(x - COL_PAD, 8), :]
            found.append((at(f, y + j, h, x) + total) - here * column[j + 1])
        return found

    arrived(u0)
    sweep(ua, ub, 0, own, f, r, ROW_PAD, ny)
    u1 = send("u1", ub, ub)
    coarse_mass = send("cr", cr, cr)
    f3 = send("f3", f, f)
    r3 = send("r3", r, r)
    for copy in u0:
        copy.wait_send()
    arrived(f2)
    arrived(r2)
    arrived(u1)
    sweep(ub, ua, 2, windows(COL_PAD, nx, 2), f, r, ROW_PAD, ny)
    sweep(ua, uc, 1, windows(COL_PAD, nx, 1), f, r, ROW_PAD, ny)

    def defect(y, carry):
        for h in range(halves):
            for k, x in enumerate(own):
                a, b, c, e = left_over(uc, ROW_PAD + RATIO * y, h, x)
                sums[y, h, pl.ds(8 * k, 8), :] = (a + b) + (c + e)
        return carry
    lax.fori_loop(0, cy, defect, 0)

    def keep_load(y, h, g, total):
        cl[DEEP + y, h, pl.ds(COARSE_PAD + 8 * g, 8), :] = total
    coarse_sums(sums, keep_load)
    coarse_load = send("cl", cl, cl)
    u3 = send("u3", uc, ud)

    arrived(coarse_mass)
    arrived(coarse_load)

    def first_coarse(y, carry):
        for h in range(halves):
            for x in windows(COARSE_PAD, cx, DEEP):
                ca[y, h, pl.ds(x, 8), :] = at(cr, y, h, x) * at(cl, y, h, x)
        return carry
    lax.fori_loop(0, cy + 2 * DEEP, first_coarse, 0)

    now, later = ca, cb
    for reach in range(DEEP - 1, 0, -1):
        sweep(now, later, reach, windows(COARSE_PAD, cx, reach), cl, cr, DEEP, cy)
        now, later = later, now

    def spread_row(y, carry):
        for h in range(halves):
            for w in range((cx + 2 + 7) // 8):
                c = at(now, DEEP - 1 + y, h, COARSE_PAD - 1 + 8 * w)
                for k in range(RATIO):
                    spread[y, h, pl.ds(32 * w + k, 8, stride=4), :] = c
        return carry
    lax.fori_loop(0, cy + 2, spread_row, 0)

    arrived(f3)
    arrived(r3)
    arrived(u3)

    def correct(y, carry):
        for h in range(halves):
            for x in own:
                add = spread[y, h, pl.ds(x - COL_PAD + 4, 8), :]
                for j in range(RATIO):
                    ua[RATIO * y + j, h, pl.ds(x, 8), :] = at(uc, RATIO * y + j, h, x) + add
            for x in (COL_PAD - 4, COL_PAD + nx):
                add = spread[y, h, pl.ds(x - COL_PAD + 4, 4), :]
                for j in range(RATIO):
                    ua[RATIO * y + j, h, pl.ds(x, 4), :] = ud[RATIO * y + j, h, pl.ds(x, 4), :] + add
        return carry
    lax.fori_loop(1, cy + 1, correct, 0)

    for y in (0, cy + 1):
        def correct_edge(j, carry):
            for h in range(halves):
                for x in windows(COL_PAD, nx, 4):
                    add = spread[y, h, pl.ds(x - COL_PAD + 4, 8), :]
                    ua[RATIO * y + j, h, pl.ds(x, 8), :] = at(ud, RATIO * y + j, h, x) + add
            return carry
        lax.fori_loop(0, RATIO, correct_edge, 0)

    for copy in u1:
        copy.wait_send()
    sweep(ua, ub, 3, windows(COL_PAD, nx, 3), f, r, ROW_PAD, ny)
    sweep(ub, ua, 2, windows(COL_PAD, nx, 2), f, r, ROW_PAD, ny)
    sweep(ua, ub, 1, windows(COL_PAD, nx, 1), f, r, ROW_PAD, ny)

    def stores(k, ref, hbm, y, rows):
        made = []
        for h in range(halves):
            made.append(pltpu.make_async_copy(
                ref.at[pl.ds(ROW_PAD + y, rows), h, pl.ds(COL_PAD, nx), :],
                hbm.at[pl.ds(y, rows), :, pl.ds(h * LANES, LANES)],
                store_sem.at[k * halves + h]))
        for copy in made:
            copy.start()
        return made

    going = stores(0, ub, improved_hbm, 0, ny)
    parts = 4
    for part in range(parts):
        def remain(y, carry):
            for h in range(halves):
                for x in own:
                    for j, found in enumerate(left_over(ub, ROW_PAD + RATIO * y, h, x)):
                        ua[ROW_PAD + RATIO * y + j, h, pl.ds(x, 8), :] = found
            return carry
        lax.fori_loop(part * cy // parts, (part + 1) * cy // parts, remain, 0)
        going += stores(1 + part, ua, remaining_hbm, part * ny // parts, ny // parts)

    for name, made in sent:
        if name not in ("u0", "u1"):
            for copy in made:
                copy.wait_send()
    for copy in going:
        copy.wait()


def local(n_row, n_col, source_terms, initial_values, absorption):
    ny, nx, layers = source_terms.shape
    halves = layers // LANES
    sizes = (ny, nx, halves, n_row, n_col)
    _, _, count = plan(ny, nx)
    fine = pltpu.VMEM((ny + 2 * ROW_PAD, halves, nx + 2 * COL_PAD, LANES), jnp.float32)
    block = pltpu.VMEM((ny, halves, nx, LANES), jnp.float32)
    cy, cx = ny // RATIO, nx // RATIO
    coarse = pltpu.VMEM((cy + 2 * DEEP, halves, cx + 2 * COARSE_PAD, LANES), jnp.float32)
    anywhere = pl.BlockSpec(memory_space=pltpu.HBM)
    shape = jax.ShapeDtypeStruct(source_terms.shape, jnp.float32)
    return pl.pallas_call(
        functools.partial(kernel, sizes),
        out_shape=(shape, shape),
        in_specs=[anywhere] * 3,
        out_specs=(anywhere, anywhere),
        scratch_shapes=[
            fine, fine, fine, fine, fine, fine, block,
            pltpu.VMEM((cy, halves, nx, LANES), jnp.float32),
            pltpu.VMEM((cy + 2, halves, (cx + 8) * RATIO, LANES), jnp.float32),
            coarse, coarse, coarse, coarse,
            pltpu.SemaphoreType.DMA((3 * halves,)),
            pltpu.SemaphoreType.DMA((5 * halves,)),
            pltpu.SemaphoreType.DMA((count,)),
            pltpu.SemaphoreType.DMA((count,)),
        ],
        compiler_params=pltpu.CompilerParams(
            collective_id=0, has_side_effects=True, vmem_limit_bytes=66_000_000
        ),
        name="two_grids",
    )(source_terms, initial_values, absorption)


def solution(mesh):
    n_row, n_col = mesh.shape["row"], mesh.shape["col"]
    spec = P("row", "col", None)
    return jax.shard_map(
        functools.partial(local, n_row, n_col),
        mesh=mesh, in_specs=(spec, spec, spec), out_specs=(spec, spec), check_vma=False,
    )
```

profile of v0, /device:TPU:2, one launch (start us, length us, event | category | flops | bytes accessed | tf_op | source)
XLA Modules:
  0.0 88.7 jit_solution(4279606597817777680)
XLA Ops:
  0.6 81.2 %two_grids.1 = (f32[64,64,256]{2,1,0:T(8,128)}, f32[64,64,256]{2,1,0:T(8,128)}) custom-call(f32[64,64,256]{2,1,0:T(8,128)} %f_hbm.1, f32[64,64,256]{2,1,0:T(8,128)} %u_hbm.1, f32[64,64,256]{2,1,0:T(8,128)} %a_hbm.1), custom_call_target="tpu_custom_call" | custom-call | tf_op jit(solution)/shard_map/two_grids/pallas_call | solution.py:327
  81.8 0.0 copy-start
  81.8 4.8 %copy.7 = f32[64,64,256]{2,1,0:T(8,128)} copy(f32[64,64,256]{2,1,0:T(8,128)} %get-tuple-element.4) | data formatting | bytes 8388608
  86.7 0.0 copy-done
  86.7 2.0 %copy.8 = f32[64,64,256]{2,1,0:T(8,128)} copy(f32[64,64,256]{2,1,0:T(8,128)S(1)} %copy-done) | data formatting | bytes 8388608
Async XLA Ops:
  81.8 4.9 %copy-start = (f32[64,64,256]{2,1,0:T(8,128)S(1)}, f32[64,64,256]{2,1,0:T(8,128)}, u32[]{:S(2)}) copy-start(f32[64,64,256]{2,1,0:T(8,128)} %get-tuple-element.5) | copy-start | bytes 12582916
where the time goes:
time: 88.8 us; the launch traced here: 88.7 us
  Pallas kernels  81.2 us (91%)
  local copies, waits for them, and re-layouts  6.87 us (8%)
    pallas_call x1, Pallas kernels, local(): pl.pallas_call(functools.partial(kernel, sizes), out_shape=(shape, shape)...  81.2 us
    unnamed x4, local copies, waits for them, and re-layouts  6.87 us

commit v1 on v0

--- a/solution.py
+++ b/solution.py
@@ -12,8 +12,9 @@
 LANES = 128
 ROW_PAD = 4
 COL_PAD = 8
-DEEP = INNER
-COARSE_PAD = 16
+FIRST = 5
+DEEP = INNER - FIRST + 1
+COARSE_PAD = 8
 MESH = pl.DeviceIdType.MESH
 
 
@@ -49,9 +50,10 @@
 def plan(ny, nx):
     rows, cols = (ROW_PAD, ny), (COL_PAD, nx)
     crows, ccols = (DEEP, ny // RATIO), (COARSE_PAD, nx // RATIO)
-    coarse = edge_rects(crows, ccols, 0, DEEP)
-    for step in range(3):
-        coarse = coarse + corner_rects(crows, ccols, 3 * step, 3 * step + 3, DEEP - 3 * step)
+    coarse = edge_rects(crows, ccols, 0, DEEP - 1)
+    coarse = coarse + corner_rects(crows, ccols, 0, 2, 4) + corner_rects(crows, ccols, 2, 4, 2)
+    values = edge_rects(crows, ccols, 0, DEEP)
+    values = values + corner_rects(crows, ccols, 0, 3, 5) + corner_rects(crows, ccols, 3, 5, 2)
     exchanges = {
         "u0": edge_rects(rows, cols, 0, 1),
         "f": edge_rects(rows, cols, 0, 2) + corner_rects(rows, cols, 0, 2, 2),
@@ -61,7 +63,8 @@
         "f3": edge_rects(rows, cols, 2, 3),
         "r3": edge_rects(rows, cols, 2, 3),
         "cl": coarse,
-        "u3": edge_rects(rows, cols, 0, 4) + corner_rects(rows, cols, 0, 3, 3),
+        "u3": edge_rects(rows, cols, 1, 4) + corner_rects(rows, cols, 0, 3, 3),
+        "cv": values,
     }
     at, first = 0, {}
     for name, rects in exchanges.items():
@@ -70,9 +73,49 @@
     return exchanges, first, at
 
 
-def kernel(sizes, f_hbm, u_hbm, a_hbm, improved_hbm, remaining_hbm,
-           ua, ub, uc, ud, f, r, d, sums, spread, cl, cr, ca, cb,
-           load_sem, store_sem, send_sem, recv_sem):
+def left_over(u, f, d, y, h, x):
+    column = [u[y + j, h, pl.ds(x, 8), :] for j in range(-1, RATIO + 1)]
+    found = []
+    for j in range(RATIO):
+        beside = u[y + j, h, pl.ds(x - 1, 8), :] + u[y + j, h, pl.ds(x + 1, 8), :]
+        total = f[y + j, h, pl.ds(x, 8), :] + ((column[j] + column[j + 2]) + beside)
+        found.append(total - d[y + j - ROW_PAD, h, pl.ds(x - COL_PAD, 8), :] * column[j + 1])
+    return found
+
+
+def finish(sizes, u, f, d, improved_hbm, remaining_hbm, left, store_sem):
+    ny, nx, halves = sizes
+    cy = ny // RATIO
+
+    def stores(k, ref, hbm, y0, x0, y, rows):
+        made = []
+        for h in range(halves):
+            made.append(pltpu.make_async_copy(
+                ref.at[pl.ds(y0 + y, rows), h, pl.ds(x0, nx), :],
+                hbm.at[pl.ds(y, rows), :, pl.ds(h * LANES, LANES)],
+                store_sem.at[k * halves + h]))
+        for copy in made:
+            copy.start()
+        return made
+
+    going = stores(0, u, improved_hbm, ROW_PAD, COL_PAD, 0, ny)
+    parts = 4
+    for part in range(parts):
+        def remain(y, carry):
+            for h in range(halves):
+                for k in range(nx // 8):
+                    for j, found in enumerate(left_over(u, f, d, ROW_PAD + RATIO * y, h, COL_PAD + 8 * k)):
+                        left[RATIO * y + j, h, pl.ds(8 * k, 8), :] = found
+            return carry
+        lax.fori_loop(part * cy // parts, (part + 1) * cy // parts, remain, 0)
+        going += stores(1 + part, left, remaining_hbm, 0, 0, part * ny // parts, ny // parts)
+    for copy in going:
+        copy.wait()
+
+
+def kernel(sizes, f_hbm, u_hbm, a_hbm, ub, f, d,
+           ua, uc, ud, r, sums, spread, cl, cr, ca, cb, cc,
+           load_sem, send_sem, recv_sem):
     ny, nx, halves, n_row, n_col = sizes
     cy, cx = ny // RATIO, nx // RATIO
     exchanges, first, _ = plan(ny, nx)
@@ -188,15 +231,6 @@
                         dst[y + j, h, pl.ds(x, 8), :] = new
             return carry
         lax.fori_loop(0, (count + 2 * reach) // step, body, 0)
-
-    def left_over(src, y, h, x):
-        column = [at(src, y + j, h, x) for j in range(-1, RATIO + 1)]
-        found = []
-        for j in range(RATIO):
-            total = (column[j] + column[j + 2]) + (at(src, y + j, h, x - 1) + at(src, y + j, h, x + 1))
-            here = d[y + j - ROW_PAD, h, pl.ds(x - COL_PAD, 8), :]
-            found.append((at(f, y + j, h, x) + total) - here * column[j + 1])
-        return found
 
     arrived(u0)
     sweep(ua, ub, 0, own, f, r, ROW_PAD, ny)
@@ -215,7 +249,7 @@
     def defect(y, carry):
         for h in range(halves):
             for k, x in enumerate(own):
-                a, b, c, e = left_over(uc, ROW_PAD + RATIO * y, h, x)
+                a, b, c, e = left_over(uc, f, d, ROW_PAD + RATIO * y, h, x)
                 sums[y, h, pl.ds(8 * k, 8), :] = (a + b) + (c + e)
         return carry
     lax.fori_loop(0, cy, defect, 0)
@@ -231,15 +265,18 @@
 
     def first_coarse(y, carry):
         for h in range(halves):
-            for x in windows(COARSE_PAD, cx, DEEP):
+            for x in windows(COARSE_PAD, cx, DEEP - 1):
                 ca[y, h, pl.ds(x, 8), :] = at(cr, y, h, x) * at(cl, y, h, x)
         return carry
-    lax.fori_loop(0, cy + 2 * DEEP, first_coarse, 0)
-
-    now, later = ca, cb
-    for reach in range(DEEP - 1, 0, -1):
-        sweep(now, later, reach, windows(COARSE_PAD, cx, reach), cl, cr, DEEP, cy)
-        now, later = later, now
+    lax.fori_loop(1, cy + 2 * DEEP - 1, first_coarse, 0)
+
+    order = [ca, cb, ca, cb, cc, ca, cb, ca, cb]
+    for k in range(1, INNER):
+        reach = FIRST - 1 - k if k < FIRST else INNER - k
+        if k == FIRST:
+            arrived(send("cv", cc, cc))
+        sweep(order[k - 1], order[k], reach, windows(COARSE_PAD, cx, reach), cl, cr, DEEP, cy)
+    now = order[-1]
 
     def spread_row(y, carry):
         for h in range(halves):
@@ -256,14 +293,14 @@
 
     def correct(y, carry):
         for h in range(halves):
-            for x in own:
+            for x in windows(COL_PAD, nx, 1):
                 add = spread[y, h, pl.ds(x - COL_PAD + 4, 8), :]
                 for j in range(RATIO):
                     ua[RATIO * y + j, h, pl.ds(x, 8), :] = at(uc, RATIO * y + j, h, x) + add
-            for x in (COL_PAD - 4, COL_PAD + nx):
-                add = spread[y, h, pl.ds(x - COL_PAD + 4, 4), :]
+            for x in (COL_PAD - 4, COL_PAD + nx + 1):
+                add = spread[y, h, pl.ds(x - COL_PAD + 4, 3), :]
                 for j in range(RATIO):
-                    ua[RATIO * y + j, h, pl.ds(x, 4), :] = ud[RATIO * y + j, h, pl.ds(x, 4), :] + add
+                    ua[RATIO * y + j, h, pl.ds(x, 3), :] = ud[RATIO * y + j, h, pl.ds(x, 3), :] + add
         return carry
     lax.fori_loop(1, cy + 1, correct, 0)
 
@@ -276,41 +313,21 @@
             return carry
         lax.fori_loop(0, RATIO, correct_edge, 0)
 
+    for y, row in ((0, ROW_PAD - 1), (cy + 1, ROW_PAD + ny)):
+        for h in range(halves):
+            for x in own:
+                ua[row, h, pl.ds(x, 8), :] = at(uc, row, h, x) + spread[y, h, pl.ds(x - COL_PAD + 4, 8), :]
+
     for copy in u1:
         copy.wait_send()
     sweep(ua, ub, 3, windows(COL_PAD, nx, 3), f, r, ROW_PAD, ny)
     sweep(ub, ua, 2, windows(COL_PAD, nx, 2), f, r, ROW_PAD, ny)
     sweep(ua, ub, 1, windows(COL_PAD, nx, 1), f, r, ROW_PAD, ny)
 
-    def stores(k, ref, hbm, y, rows):
-        made = []
-        for h in range(halves):
-            made.append(pltpu.make_async_copy(
-                ref.at[pl.ds(ROW_PAD + y, rows), h, pl.ds(COL_PAD, nx), :],
-                hbm.at[pl.ds(y, rows), :, pl.ds(h * LANES, LANES)],
-                store_sem.at[k * halves + h]))
-        for copy in made:
-            copy.start()
-        return made
-
-    going = stores(0, ub, improved_hbm, 0, ny)
-    parts = 4
-    for part in range(parts):
-        def remain(y, carry):
-            for h in range(halves):
-                for x in own:
-                    for j, found in enumerate(left_over(ub, ROW_PAD + RATIO * y, h, x)):
-                        ua[ROW_PAD + RATIO * y + j, h, pl.ds(x, 8), :] = found
-            return carry
-        lax.fori_loop(part * cy // parts, (part + 1) * cy // parts, remain, 0)
-        going += stores(1 + part, ua, remaining_hbm, part * ny // parts, ny // parts)
-
     for name, made in sent:
         if name not in ("u0", "u1"):
             for copy in made:
                 copy.wait_send()
-    for copy in going:
-        copy.wait()
 
 
 def local(n_row, n_col, source_terms, initial_values, absorption):
@@ -318,32 +335,45 @@
     halves = layers // LANES
     sizes = (ny, nx, halves, n_row, n_col)
     _, _, count = plan(ny, nx)
-    fine = pltpu.VMEM((ny + 2 * ROW_PAD, halves, nx + 2 * COL_PAD, LANES), jnp.float32)
-    block = pltpu.VMEM((ny, halves, nx, LANES), jnp.float32)
+    fine = (ny + 2 * ROW_PAD, halves, nx + 2 * COL_PAD, LANES)
+    block = (ny, halves, nx, LANES)
     cy, cx = ny // RATIO, nx // RATIO
     coarse = pltpu.VMEM((cy + 2 * DEEP, halves, cx + 2 * COARSE_PAD, LANES), jnp.float32)
+
+    def vmem(shape):
+        return pltpu.VMEM(shape, jnp.float32)
+
     anywhere = pl.BlockSpec(memory_space=pltpu.HBM)
-    shape = jax.ShapeDtypeStruct(source_terms.shape, jnp.float32)
-    return pl.pallas_call(
+    inside = pl.BlockSpec(memory_space=pltpu.VMEM)
+    u, f, d = pl.pallas_call(
         functools.partial(kernel, sizes),
-        out_shape=(shape, shape),
+        out_shape=(vmem(fine), vmem(fine), vmem(block)),
         in_specs=[anywhere] * 3,
-        out_specs=(anywhere, anywhere),
+        out_specs=(inside,) * 3,
         scratch_shapes=[
-            fine, fine, fine, fine, fine, fine, block,
-            pltpu.VMEM((cy, halves, nx, LANES), jnp.float32),
-            pltpu.VMEM((cy + 2, halves, (cx + 8) * RATIO, LANES), jnp.float32),
-            coarse, coarse, coarse, coarse,
+            vmem(fine), vmem(fine), vmem(fine), vmem(fine),
+            vmem((cy, halves, nx, LANES)),
+            vmem((cy + 2, halves, (cx + 8) * RATIO, LANES)),
+            coarse, coarse, coarse, coarse, coarse,
             pltpu.SemaphoreType.DMA((3 * halves,)),
-            pltpu.SemaphoreType.DMA((5 * halves,)),
             pltpu.SemaphoreType.DMA((count,)),
             pltpu.SemaphoreType.DMA((count,)),
         ],
         compiler_params=pltpu.CompilerParams(
-            collective_id=0, has_side_effects=True, vmem_limit_bytes=66_000_000
+            collective_id=0, has_side_effects=True, vmem_limit_bytes=44_000_000
         ),
         name="two_grids",
     )(source_terms, initial_values, absorption)
+    shape = jax.ShapeDtypeStruct(source_terms.shape, jnp.float32)
+    return pl.pallas_call(
+        functools.partial(finish, (ny, nx, halves)),
+        out_shape=(shape, shape),
+        in_specs=[inside] * 3,
+        out_specs=(anywhere, anywhere),
+        scratch_shapes=[vmem(block), pltpu.SemaphoreType.DMA((5 * halves,))],
+        compiler_params=pltpu.CompilerParams(vmem_limit_bytes=8_000_000),
+        name="finish",
+    )(u, f, d)
 
 
 def solution(mesh):

time: 88.8 us -> 79.5 us (0.90)
  the two profiles are of different devices: /device:TPU:2 before, /device:TPU:1 now
where the time goes in v1:
time: 79.5 us; the launch traced here: 79.4 us
  Pallas kernels  78.8 us (99%)
    pallas_call x1, Pallas kernels, local(): pl.pallas_call(functools.partial(kernel, sizes), out_shape=(vmem(fine), v...  75.4 us
    pallas_call x1, Pallas kernels, local(): pl.pallas_call(functools.partial(finish, (ny, nx, halves)), out_shape=(sh...  3.37 us

profile of v1, /device:TPU:1, one launch (start us, length us, event | category | flops | bytes accessed | tf_op | source)
XLA Modules:
  0.0 79.4 jit_solution(15708136988146585256)
XLA Ops:
  0.6 75.4 %two_grids.1 = (f32[72,2,80,128]{3,2,1,0:T(8,128)S(1)}, f32[72,2,80,128]{3,2,1,0:T(8,128)S(1)}, f32[64,2,64,128]{3,2,1,0:T(8,128)S(1)}) custom-call(f32[64,64,256]{2,1,0:T(8,128)} %f_hbm.1, f32[64,64,256]{2,1,0:T(8,128)} %u_hbm.1, f32[64,64,256]{2,1,0:T(8,128)} %a_hbm.1), custom_call_target="tpu_custom_call" | custom-call | tf_op jit(solution)/shard_map/two_grids/pallas_call | solution.py:348
  76.0 3.4 %finish.1 = (f32[64,64,256]{2,1,0:T(8,128)}, f32[64,64,256]{2,1,0:T(8,128)}) custom-call(f32[72,2,80,128]{3,2,1,0:T(8,128)S(1)} %get-tuple-element.5.u, f32[72,2,80,128]{3,2,1,0:T(8,128)S(1)} %get-tuple-element.6.f, f32[64,2,64,128]{3,2,1,0:T(8,128)S(1)} %get-tuple-element.7.d), custom_call_target="tpu_custom_call" | custom-call | tf_op jit(solution)/shard_map/finish/pallas_call | solution.py:368

commit v2 on v1

--- a/solution.py
+++ b/solution.py
@@ -113,8 +113,8 @@
         copy.wait()
 
 
-def kernel(sizes, f_hbm, u_hbm, a_hbm, ub, f, d,
-           ua, uc, ud, r, sums, spread, cl, cr, ca, cb, cc,
+def kernel(sizes, f_hbm, u_hbm, a_hbm, ud, f, d,
+           ua, ub, uc, r, sums, spread, cl, cr, ca, cb, cc,
            load_sem, send_sem, recv_sem):
     ny, nx, halves, n_row, n_col = sizes
     cy, cx = ny // RATIO, nx // RATIO
@@ -219,9 +219,11 @@
     f2 = send("f", f, f)
     r2 = send("r", r, r)
 
-    def sweep(src, dst, reach, starts, load, rate, top, count, step=2):
+    def region(src, dst, y0, y1, starts, load, rate):
+        step = next(k for k in (2, 3, 1) if (y1 - y0) % k == 0)
+
         def body(i, carry):
-            y = top - reach + step * i
+            y = y0 + step * i
             for h in range(halves):
                 for x in starts:
                     column = [at(src, y + j, h, x) for j in range(-1, step + 1)]
@@ -230,29 +232,46 @@
                         new = 0.2 * column[j + 1] + at(rate, y + j, h, x) * (at(load, y + j, h, x) + total)
                         dst[y + j, h, pl.ds(x, 8), :] = new
             return carry
-        lax.fori_loop(0, (count + 2 * reach) // step, body, 0)
-
+        lax.fori_loop(0, (y1 - y0) // step, body, 0)
+
+    def interior(src, dst, inset):
+        region(src, dst, ROW_PAD + inset, ROW_PAD + ny - inset, windows(COL_PAD, nx, -inset), f, r)
+
+    def frame(src, dst, inset, reach):
+        low, high = ROW_PAD + inset, ROW_PAD + ny - inset
+        full = windows(COL_PAD, nx, reach)
+        region(src, dst, ROW_PAD - reach, low, full, f, r)
+        region(src, dst, high, ROW_PAD + ny + reach, full, f, r)
+        region(src, dst, low, high, [full[0], full[-1]], f, r)
+
+    def defect(y0, y1, starts):
+        def body(y, carry):
+            for h in range(halves):
+                for x in starts:
+                    a, b, c, e = left_over(uc, f, d, ROW_PAD + RATIO * y, h, x)
+                    sums[y, h, pl.ds(x - COL_PAD, 8), :] = (a + b) + (c + e)
+            return carry
+        lax.fori_loop(y0, y1, body, 0)
+
+    interior(ua, ub, 1)
     arrived(u0)
-    sweep(ua, ub, 0, own, f, r, ROW_PAD, ny)
+    frame(ua, ub, 1, 0)
     u1 = send("u1", ub, ub)
     coarse_mass = send("cr", cr, cr)
-    f3 = send("f3", f, f)
-    r3 = send("r3", r, r)
     for copy in u0:
         copy.wait_send()
+
+    interior(ub, ua, 1)
+    interior(ua, uc, 2)
+    defect(1, cy - 1, own[1:-1])
     arrived(f2)
     arrived(r2)
     arrived(u1)
-    sweep(ub, ua, 2, windows(COL_PAD, nx, 2), f, r, ROW_PAD, ny)
-    sweep(ua, uc, 1, windows(COL_PAD, nx, 1), f, r, ROW_PAD, ny)
-
-    def defect(y, carry):
-        for h in range(halves):
-            for k, x in enumerate(own):
-                a, b, c, e = left_over(uc, f, d, ROW_PAD + RATIO * y, h, x)
-                sums[y, h, pl.ds(8 * k, 8), :] = (a + b) + (c + e)
-        return carry
-    lax.fori_loop(0, cy, defect, 0)
+    frame(ub, ua, 1, 2)
+    frame(ua, uc, 2, 1)
+    defect(0, 1, own)
+    defect(cy - 1, cy, own)
+    defect(1, cy - 1, [own[0], own[-1]])
 
     def keep_load(y, h, g, total):
         cl[DEEP + y, h, pl.ds(COARSE_PAD + 8 * g, 8), :] = total
@@ -274,8 +293,11 @@
     for k in range(1, INNER):
         reach = FIRST - 1 - k if k < FIRST else INNER - k
         if k == FIRST:
-            arrived(send("cv", cc, cc))
-        sweep(order[k - 1], order[k], reach, windows(COARSE_PAD, cx, reach), cl, cr, DEEP, cy)
+            coarse_values = send("cv", cc, cc)
+            f3 = send("f3", f, f)
+            r3 = send("r3", r, r)
+            arrived(coarse_values)
+        region(order[k - 1], order[k], DEEP - reach, DEEP + cy + reach, windows(COARSE_PAD, cx, reach), cl, cr)
     now = order[-1]
 
     def spread_row(y, carry):
@@ -287,22 +309,37 @@
         return carry
     lax.fori_loop(0, cy + 2, spread_row, 0)
 
-    arrived(f3)
-    arrived(r3)
-    arrived(u3)
-
     def correct(y, carry):
         for h in range(halves):
-            for x in windows(COL_PAD, nx, 1):
+            for x in own:
                 add = spread[y, h, pl.ds(x - COL_PAD + 4, 8), :]
                 for j in range(RATIO):
                     ua[RATIO * y + j, h, pl.ds(x, 8), :] = at(uc, RATIO * y + j, h, x) + add
+        return carry
+    lax.fori_loop(1, cy + 1, correct, 0)
+
+    for copy in u1:
+        copy.wait_send()
+    interior(ua, ub, 1)
+    for copy in u3:
+        copy.wait_send()
+    interior(ub, uc, 2)
+    interior(uc, ud, 3)
+
+    arrived(u3)
+
+    def correct_sides(y, carry):
+        for h in range(halves):
             for x in (COL_PAD - 4, COL_PAD + nx + 1):
                 add = spread[y, h, pl.ds(x - COL_PAD + 4, 3), :]
                 for j in range(RATIO):
                     ua[RATIO * y + j, h, pl.ds(x, 3), :] = ud[RATIO * y + j, h, pl.ds(x, 3), :] + add
+            for x in (COL_PAD - 1, COL_PAD + nx):
+                add = spread[y, h, pl.ds(x - COL_PAD + 4, 1), :]
+                for j in range(RATIO):
+                    ua[RATIO * y + j, h, pl.ds(x, 1), :] = uc[RATIO * y + j, h, pl.ds(x, 1), :] + add
         return carry
-    lax.fori_loop(1, cy + 1, correct, 0)
+    lax.fori_loop(1, cy + 1, correct_sides, 0)
 
     for y in (0, cy + 1):
         def correct_edge(j, carry):
@@ -318,14 +355,14 @@
             for x in own:
                 ua[row, h, pl.ds(x, 8), :] = at(uc, row, h, x) + spread[y, h, pl.ds(x - COL_PAD + 4, 8), :]
 
-    for copy in u1:
-        copy.wait_send()
-    sweep(ua, ub, 3, windows(COL_PAD, nx, 3), f, r, ROW_PAD, ny)
-    sweep(ub, ua, 2, windows(COL_PAD, nx, 2), f, r, ROW_PAD, ny)
-    sweep(ua, ub, 1, windows(COL_PAD, nx, 1), f, r, ROW_PAD, ny)
+    arrived(f3)
+    arrived(r3)
+    frame(ua, ub, 1, 3)
+    frame(ub, uc, 2, 2)
+    frame(uc, ud, 3, 1)
 
     for name, made in sent:
-        if name not in ("u0", "u1"):
+        if name not in ("u0", "u1", "u3"):
             for copy in made:
                 copy.wait_send()
 

time: 79.5 us -> 77.9 us (0.980)
  Pallas kernels: 78.8 us -> 77.2 us
    pallas_call x1, Pallas kernels: 75.4 us -> 73.8 us  [local(): pl.pallas_call(functools.partial(kernel, sizes), out_shape=(vmem(fine), v...]
where the time goes in v2:
time: 77.9 us; the launch traced here: 77.8 us
  Pallas kernels  77.2 us (99%)
    pallas_call x1, Pallas kernels, local(): pl.pallas_call(functools.partial(kernel, sizes), out_shape=(vmem(fine), v...  73.8 us
    pallas_call x1, Pallas kernels, local(): pl.pallas_call(functools.partial(finish, (ny, nx, halves)), out_shape=(sh...  3.37 us

profile of v2, /device:TPU:1, one launch (start us, length us, event | category | flops | bytes accessed | tf_op | source)
XLA Modules:
  0.0 77.8 jit_solution(8688561015260455346)
XLA Ops:
  0.6 73.8 %two_grids.1 = (f32[72,2,80,128]{3,2,1,0:T(8,128)S(1)}, f32[72,2,80,128]{3,2,1,0:T(8,128)S(1)}, f32[64,2,64,128]{3,2,1,0:T(8,128)S(1)}) custom-call(f32[64,64,256]{2,1,0:T(8,128)} %f_hbm.1, f32[64,64,256]{2,1,0:T(8,128)} %u_hbm.1, f32[64,64,256]{2,1,0:T(8,128)} %a_hbm.1), custom_call_target="tpu_custom_call" | custom-call | tf_op jit(solution)/shard_map/two_grids/pallas_call | solution.py:385
  74.5 3.4 %finish.1 = (f32[64,64,256]{2,1,0:T(8,128)}, f32[64,64,256]{2,1,0:T(8,128)}) custom-call(f32[72,2,80,128]{3,2,1,0:T(8,128)S(1)} %get-tuple-element.5.u, f32[72,2,80,128]{3,2,1,0:T(8,128)S(1)} %get-tuple-element.6.f, f32[64,2,64,128]{3,2,1,0:T(8,128)S(1)} %get-tuple-element.7.d), custom_call_target="tpu_custom_call" | custom-call | tf_op jit(solution)/shard_map/finish/pallas_call | solution.py:405

commit v3 on v2

--- a/solution.py
+++ b/solution.py
@@ -55,15 +55,15 @@
     values = edge_rects(crows, ccols, 0, DEEP)
     values = values + corner_rects(crows, ccols, 0, 3, 5) + corner_rects(crows, ccols, 3, 5, 2)
     exchanges = {
-        "u0": edge_rects(rows, cols, 0, 1),
-        "f": edge_rects(rows, cols, 0, 2) + corner_rects(rows, cols, 0, 2, 2),
-        "r": edge_rects(rows, cols, 0, 2) + corner_rects(rows, cols, 0, 2, 2),
-        "u1": edge_rects(rows, cols, 0, 3) + corner_rects(rows, cols, 0, 2, 2),
+        "u0": edge_rects(rows, cols, 0, 2) + corner_rects(rows, cols, 0, 1, 1),
+        "f": edge_rects(rows, cols, 0, 1),
+        "r": edge_rects(rows, cols, 0, 1),
+        "r3": edge_rects(rows, cols, 1, 3) + corner_rects(rows, cols, 0, 2, 2),
+        "u2": edge_rects(rows, cols, 0, 2) + corner_rects(rows, cols, 0, 1, 1),
         "cr": coarse,
-        "f3": edge_rects(rows, cols, 2, 3),
-        "r3": edge_rects(rows, cols, 2, 3),
         "cl": coarse,
-        "u3": edge_rects(rows, cols, 1, 4) + corner_rects(rows, cols, 0, 3, 3),
+        "v4": edge_rects(rows, cols, 0, 2) + corner_rects(rows, cols, 0, 1, 1),
+        "v6": edge_rects(rows, cols, 0, 1),
         "cv": values,
     }
     at, first = 0, {}
@@ -113,8 +113,8 @@
         copy.wait()
 
 
-def kernel(sizes, f_hbm, u_hbm, a_hbm, ud, f, d,
-           ua, ub, uc, r, sums, spread, cl, cr, ca, cb, cc,
+def kernel(sizes, f_hbm, u_hbm, a_hbm, ua, f, d,
+           ub, uc, ud, ue, r, sums, spread, cl, cr, ca, cb, cc,
            load_sem, send_sem, recv_sem):
     ny, nx, halves, n_row, n_col = sizes
     cy, cx = ny // RATIO, nx // RATIO
@@ -216,8 +216,9 @@
     u0 = send("u0", ua, ua)
     for copy in f_loads:
         copy.wait()
-    f2 = send("f", f, f)
-    r2 = send("r", r, r)
+    f1 = send("f", f, f)
+    r1 = send("r", r, r)
+    r3 = send("r3", r, r)
 
     def region(src, dst, y0, y1, starts, load, rate):
         step = next(k for k in (2, 3, 1) if (y1 - y0) % k == 0)
@@ -238,37 +239,37 @@
         region(src, dst, ROW_PAD + inset, ROW_PAD + ny - inset, windows(COL_PAD, nx, -inset), f, r)
 
     def frame(src, dst, inset, reach):
-        low, high = ROW_PAD + inset, ROW_PAD + ny - inset
         full = windows(COL_PAD, nx, reach)
-        region(src, dst, ROW_PAD - reach, low, full, f, r)
-        region(src, dst, high, ROW_PAD + ny + reach, full, f, r)
-        region(src, dst, low, high, [full[0], full[-1]], f, r)
+        region(src, dst, ROW_PAD - reach, ROW_PAD + inset, own, f, r)
+        region(src, dst, ROW_PAD + ny - inset, ROW_PAD + ny + reach, own, f, r)
+        region(src, dst, ROW_PAD, ROW_PAD + ny, [full[0], full[-1]], f, r)
 
     def defect(y0, y1, starts):
         def body(y, carry):
             for h in range(halves):
                 for x in starts:
-                    a, b, c, e = left_over(uc, f, d, ROW_PAD + RATIO * y, h, x)
+                    a, b, c, e = left_over(ua, f, d, ROW_PAD + RATIO * y, h, x)
                     sums[y, h, pl.ds(x - COL_PAD, 8), :] = (a + b) + (c + e)
             return carry
         lax.fori_loop(y0, y1, body, 0)
 
     interior(ua, ub, 1)
+    interior(ub, uc, 2)
     arrived(u0)
-    frame(ua, ub, 1, 0)
-    u1 = send("u1", ub, ub)
+    arrived(f1)
+    arrived(r1)
+    frame(ua, ub, 1, 1)
+    frame(ub, uc, 2, 0)
+    u2 = send("u2", uc, uc)
     coarse_mass = send("cr", cr, cr)
     for copy in u0:
         copy.wait_send()
 
-    interior(ub, ua, 1)
-    interior(ua, uc, 2)
+    interior(uc, ua, 1)
     defect(1, cy - 1, own[1:-1])
-    arrived(f2)
-    arrived(r2)
-    arrived(u1)
-    frame(ub, ua, 1, 2)
-    frame(ua, uc, 2, 1)
+    interior(ua, ud, 2)
+    arrived(u2)
+    frame(uc, ua, 1, 1)
     defect(0, 1, own)
     defect(cy - 1, cy, own)
     defect(1, cy - 1, [own[0], own[-1]])
@@ -277,7 +278,11 @@
         cl[DEEP + y, h, pl.ds(COARSE_PAD + 8 * g, 8), :] = total
     coarse_sums(sums, keep_load)
     coarse_load = send("cl", cl, cl)
-    u3 = send("u3", uc, ud)
+    frame(ua, ud, 2, 0)
+    v4 = send("v4", ud, ud)
+
+    interior(ud, ub, 1)
+    interior(ub, ue, 2)
 
     arrived(coarse_mass)
     arrived(coarse_load)
@@ -294,8 +299,10 @@
         reach = FIRST - 1 - k if k < FIRST else INNER - k
         if k == FIRST:
             coarse_values = send("cv", cc, cc)
-            f3 = send("f3", f, f)
-            r3 = send("r3", r, r)
+            arrived(v4)
+            frame(ud, ub, 1, 1)
+            frame(ub, ue, 2, 0)
+            v6 = send("v6", ue, ue)
             arrived(coarse_values)
         region(order[k - 1], order[k], DEEP - reach, DEEP + cy + reach, windows(COARSE_PAD, cx, reach), cl, cr)
     now = order[-1]
@@ -309,60 +316,58 @@
         return carry
     lax.fori_loop(0, cy + 2, spread_row, 0)
 
-    def correct(y, carry):
-        for h in range(halves):
-            for x in own:
-                add = spread[y, h, pl.ds(x - COL_PAD + 4, 8), :]
-                for j in range(RATIO):
-                    ua[RATIO * y + j, h, pl.ds(x, 8), :] = at(uc, RATIO * y + j, h, x) + add
+    arrived(r3)
+    for copy in u2:
+        copy.wait_send()
+
+    def swept(y, rows, starts):
+        for h in range(halves):
+            for x in starts:
+                e = x - COL_PAD + 4
+                here = spread[y, h, pl.ds(e, 8), :]
+                beside = spread[y, h, pl.ds(e - 1, 8), :] + spread[y, h, pl.ds(e + 1, 8), :]
+                kept = 0.2 * here
+                for j in rows:
+                    if j == 0:
+                        total = beside + (here + spread[y - 1, h, pl.ds(e, 8), :])
+                    elif j == RATIO - 1:
+                        total = beside + (here + spread[y + 1, h, pl.ds(e, 8), :])
+                    else:
+                        total = beside + (here + here)
+                    uc[RATIO * y + j, h, pl.ds(x, 8), :] = kept + at(r, RATIO * y + j, h, x) * total
+
+    reach3 = windows(COL_PAD, nx, 3)
+
+    def first_swept(y, carry):
+        swept(y, range(RATIO), reach3)
         return carry
-    lax.fori_loop(1, cy + 1, correct, 0)
-
-    for copy in u1:
-        copy.wait_send()
-    interior(ua, ub, 1)
-    for copy in u3:
-        copy.wait_send()
-    interior(ub, uc, 2)
-    interior(uc, ud, 3)
-
-    arrived(u3)
-
-    def correct_sides(y, carry):
-        for h in range(halves):
-            for x in (COL_PAD - 4, COL_PAD + nx + 1):
-                add = spread[y, h, pl.ds(x - COL_PAD + 4, 3), :]
-                for j in range(RATIO):
-                    ua[RATIO * y + j, h, pl.ds(x, 3), :] = ud[RATIO * y + j, h, pl.ds(x, 3), :] + add
-            for x in (COL_PAD - 1, COL_PAD + nx):
-                add = spread[y, h, pl.ds(x - COL_PAD + 4, 1), :]
-                for j in range(RATIO):
-                    ua[RATIO * y + j, h, pl.ds(x, 1), :] = uc[RATIO * y + j, h, pl.ds(x, 1), :] + add
-        return carry
-    lax.fori_loop(1, cy + 1, correct_sides, 0)
-
-    for y in (0, cy + 1):
-        def correct_edge(j, carry):
+    lax.fori_loop(1, cy + 1, first_swept, 0)
+    swept(0, range(1, RATIO), reach3)
+    swept(cy + 1, range(RATIO - 1), reach3)
+
+    def sweep_correction(src, dst, reach, base):
+        starts = windows(COL_PAD, nx, reach)
+
+        def body(i, carry):
+            y = ROW_PAD - reach + 2 * i
             for h in range(halves):
-                for x in windows(COL_PAD, nx, 4):
-                    add = spread[y, h, pl.ds(x - COL_PAD + 4, 8), :]
-                    ua[RATIO * y + j, h, pl.ds(x, 8), :] = at(ud, RATIO * y + j, h, x) + add
+                for x in starts:
+                    column = [at(src, y + j, h, x) for j in range(-1, 3)]
+                    for j in range(2):
+                        total = (column[j] + column[j + 2]) + (at(src, y + j, h, x - 1) + at(src, y + j, h, x + 1))
+                        new = 0.2 * column[j + 1] + at(r, y + j, h, x) * total
+                        if base is not None:
+                            new = at(base, y + j, h, x) + new
+                        dst[y + j, h, pl.ds(x, 8), :] = new
             return carry
-        lax.fori_loop(0, RATIO, correct_edge, 0)
-
-    for y, row in ((0, ROW_PAD - 1), (cy + 1, ROW_PAD + ny)):
-        for h in range(halves):
-            for x in own:
-                ua[row, h, pl.ds(x, 8), :] = at(uc, row, h, x) + spread[y, h, pl.ds(x - COL_PAD + 4, 8), :]
-
-    arrived(f3)
-    arrived(r3)
-    frame(ua, ub, 1, 3)
-    frame(ub, uc, 2, 2)
-    frame(uc, ud, 3, 1)
+        lax.fori_loop(0, (ny + 2 * reach) // 2, body, 0)
+
+    sweep_correction(uc, ub, 2, None)
+    arrived(v6)
+    sweep_correction(ub, ua, 1, ue)
 
     for name, made in sent:
-        if name not in ("u0", "u1", "u3"):
+        if name not in ("u0", "u2"):
             for copy in made:
                 copy.wait_send()
 
@@ -388,7 +393,7 @@
         in_specs=[anywhere] * 3,
         out_specs=(inside,) * 3,
         scratch_shapes=[
-            vmem(fine), vmem(fine), vmem(fine), vmem(fine),
+            vmem(fine), vmem(fine), vmem(fine), vmem(fine), vmem(fine),
             vmem((cy, halves, nx, LANES)),
             vmem((cy + 2, halves, (cx + 8) * RATIO, LANES)),
             coarse, coarse, coarse, coarse, coarse,

time: 77.9 us -> 64.9 us (0.83)
  Pallas kernels: 77.2 us -> 64.1 us
    pallas_call x1, Pallas kernels: 73.8 us -> 60.7 us  [local(): pl.pallas_call(functools.partial(kernel, sizes), out_shape=(vmem(fine), v...]
where the time goes in v3:
time: 64.9 us; the launch traced here: 64.7 us
  Pallas kernels  64.1 us (99%)
    pallas_call x1, Pallas kernels, local(): pl.pallas_call(functools.partial(kernel, sizes), out_shape=(vmem(fine), v...  60.7 us
    pallas_call x1, Pallas kernels, local(): pl.pallas_call(functools.partial(finish, (ny, nx, halves)), out_shape=(sh...  3.37 us

profile of v3, /device:TPU:1, one launch (start us, length us, event | category | flops | bytes accessed | tf_op | source)
XLA Modules:
  0.0 64.7 jit_solution(12547794999109401107)
XLA Ops:
  0.6 60.7 %two_grids.1 = (f32[72,2,80,128]{3,2,1,0:T(8,128)S(1)}, f32[72,2,80,128]{3,2,1,0:T(8,128)S(1)}, f32[64,2,64,128]{3,2,1,0:T(8,128)S(1)}) custom-call(f32[64,64,256]{2,1,0:T(8,128)} %f_hbm.1, f32[64,64,256]{2,1,0:T(8,128)} %u_hbm.1, f32[64,64,256]{2,1,0:T(8,128)} %a_hbm.1), custom_call_target="tpu_custom_call" | custom-call | tf_op jit(solution)/shard_map/two_grids/pallas_call | solution.py:390
  61.4 3.4 %finish.1 = (f32[64,64,256]{2,1,0:T(8,128)}, f32[64,64,256]{2,1,0:T(8,128)}) custom-call(f32[72,2,80,128]{3,2,1,0:T(8,128)S(1)} %get-tuple-element.5.u, f32[72,2,80,128]{3,2,1,0:T(8,128)S(1)} %get-tuple-element.6.f, f32[64,2,64,128]{3,2,1,0:T(8,128)S(1)} %get-tuple-element.7.d), custom_call_target="tpu_custom_call" | custom-call | tf_op jit(solution)/shard_map/finish/pallas_call | solution.py:410

commit v4 on v3

--- a/solution.py
+++ b/solution.py
@@ -83,7 +83,23 @@
     return found
 
 
-def finish(sizes, u, f, d, improved_hbm, remaining_hbm, left, store_sem):
+def windows(x0, n, reach):
+    low, high = x0 - reach, x0 + n + reach
+    return [min(x, high - 8) for x in range(low, high, 8)]
+
+
+def swept_twice(src, r, base, dst, y, h, x):
+    column = [src[y + j, h, pl.ds(x, 8), :] for j in range(-1, 3)]
+    for j in range(2):
+        beside = src[y + j, h, pl.ds(x - 1, 8), :] + src[y + j, h, pl.ds(x + 1, 8), :]
+        total = (column[j] + column[j + 2]) + beside
+        new = 0.2 * column[j + 1] + r[y + j, h, pl.ds(x, 8), :] * total
+        if base is not None:
+            new = base[y + j, h, pl.ds(x, 8), :] + new
+        dst[y + j, h, pl.ds(x, 8), :] = new
+
+
+def finish(sizes, e, v, f, d, r, improved_hbm, remaining_hbm, u, left, store_sem):
     ny, nx, halves = sizes
     cy = ny // RATIO
 
@@ -98,9 +114,21 @@
             copy.start()
         return made
 
-    going = stores(0, u, improved_hbm, ROW_PAD, COL_PAD, 0, ny)
+    going = []
     parts = 4
+    starts = windows(COL_PAD, nx, 1)
+    rows = ny // parts
     for part in range(parts):
+        low = part * rows + 1 if part else -1
+
+        def last(i, carry):
+            for h in range(halves):
+                for x in starts:
+                    swept_twice(e, r, v, u, ROW_PAD + low + 2 * i, h, x)
+            return carry
+        lax.fori_loop(0, ((part + 1) * rows + 1 - low) // 2, last, 0)
+        going += stores(2 * part, u, improved_hbm, ROW_PAD, COL_PAD, part * rows, rows)
+
         def remain(y, carry):
             for h in range(halves):
                 for k in range(nx // 8):
@@ -108,13 +136,13 @@
                         left[RATIO * y + j, h, pl.ds(8 * k, 8), :] = found
             return carry
         lax.fori_loop(part * cy // parts, (part + 1) * cy // parts, remain, 0)
-        going += stores(1 + part, left, remaining_hbm, 0, 0, part * ny // parts, ny // parts)
+        going += stores(2 * part + 1, left, remaining_hbm, 0, 0, part * ny // parts, ny // parts)
     for copy in going:
         copy.wait()
 
 
-def kernel(sizes, f_hbm, u_hbm, a_hbm, ua, f, d,
-           ub, uc, ud, ue, r, sums, spread, cl, cr, ca, cb, cc,
+def kernel(sizes, f_hbm, u_hbm, a_hbm, ub, ue, f, d, r,
+           ua, uc, ud, sums, spread, cl, cr, ca, cb, cc,
            load_sem, send_sem, recv_sem):
     ny, nx, halves, n_row, n_col = sizes
     cy, cx = ny // RATIO, nx // RATIO
@@ -131,24 +159,47 @@
     def copies(name, source, landing):
         made = []
         for k, (dy, dx, src, dst) in enumerate(exchanges[name]):
-            made.append(pltpu.make_async_remote_copy(
+            made.append((pltpu.make_async_remote_copy(
                 src_ref=box(source, src), dst_ref=box(landing, dst),
                 send_sem=send_sem.at[first[name] + k], recv_sem=recv_sem.at[first[name] + k],
-                device_id=neighbour(dy, dx), device_id_type=MESH))
+                device_id=neighbour(dy, dx), device_id_type=MESH), dx == 0))
         return made
 
     sent = []
 
-    def send(name, source, landing):
-        made = copies(name, source, landing)
-        for copy in made:
+    def send(*given):
+        found = [copies(*one) for one in given]
+        sent.extend(found)
+        return found
+
+    def along(made, y_only):
+        return [copy for part in made for copy, is_y in part if is_y == y_only]
+
+    def start_x(made):
+        for copy in along(made, False):
             copy.start()
-        sent.append((name, made))
-        return made
+
+    def start_y(made):
+        for copy in along(made, True):
+            copy.start()
+
+    def gone_x(made):
+        for copy in along(made, False):
+            copy.wait_send()
+
+    def gone_y(made):
+        for copy in along(made, True):
+            copy.wait_send()
 
     def arrived(made):
-        for copy in made:
-            copy.wait_recv()
+        for part in made:
+            for copy, _ in part:
+                copy.wait_recv()
+
+    barrier = pltpu.get_barrier_semaphore()
+    around = [(dy, dx) for dy in (-1, 0, 1) for dx in (-1, 0, 1) if (dy, dx) != (0, 0)]
+    for dy, dx in around:
+        pl.semaphore_signal(barrier, inc=1, device_id=neighbour(dy, dx), device_id_type=MESH)
 
     def loads(k, hbm, ref, y0, x0):
         made = []
@@ -165,16 +216,7 @@
     u_loads = loads(1, u_hbm, ua, ROW_PAD, COL_PAD)
     f_loads = loads(2, f_hbm, f, ROW_PAD, COL_PAD)
 
-    barrier = pltpu.get_barrier_semaphore()
-    around = [(dy, dx) for dy in (-1, 0, 1) for dx in (-1, 0, 1) if (dy, dx) != (0, 0)]
-    for dy, dx in around:
-        pl.semaphore_signal(barrier, inc=1, device_id=neighbour(dy, dx), device_id_type=MESH)
-
     own = [COL_PAD + 8 * k for k in range(nx // 8)]
-
-    def windows(x0, n, reach):
-        low, high = x0 - reach, x0 + n + reach
-        return [min(x, high - 8) for x in range(low, high, 8)]
 
     def at(ref, y, h, x):
         return ref[y, h, pl.ds(x, 8), :]
@@ -213,12 +255,10 @@
     pl.semaphore_wait(barrier, len(around))
     for copy in u_loads:
         copy.wait()
-    u0 = send("u0", ua, ua)
     for copy in f_loads:
         copy.wait()
-    f1 = send("f", f, f)
-    r1 = send("r", r, r)
-    r3 = send("r3", r, r)
+    start = send(("u0", ua, ua), ("f", f, f), ("r", r, r))
+    start_x(start)
 
     def region(src, dst, y0, y1, starts, load, rate):
         step = next(k for k in (2, 3, 1) if (y1 - y0) % k == 0)
@@ -255,18 +295,25 @@
 
     interior(ua, ub, 1)
     interior(ub, uc, 2)
-    arrived(u0)
-    arrived(f1)
-    arrived(r1)
+    gone_x(start)
+    start_y(start)
+    r3 = send(("r3", r, r))
+    gone_y(start)
+    start_x(r3)
+    arrived(start)
     frame(ua, ub, 1, 1)
     frame(ub, uc, 2, 0)
-    u2 = send("u2", uc, uc)
-    coarse_mass = send("cr", cr, cr)
-    for copy in u0:
-        copy.wait_send()
+    u2 = send(("u2", uc, uc))
+    start_x(u2)
 
     interior(uc, ua, 1)
     defect(1, cy - 1, own[1:-1])
+    gone_x(u2)
+    start_y(u2)
+    coarse_mass = send(("cr", cr, cr))
+    start_x(coarse_mass)
+    start_y(coarse_mass)
+    start_y(r3)
     interior(ua, ud, 2)
     arrived(u2)
     frame(uc, ua, 1, 1)
@@ -277,11 +324,16 @@
     def keep_load(y, h, g, total):
         cl[DEEP + y, h, pl.ds(COARSE_PAD + 8 * g, 8), :] = total
     coarse_sums(sums, keep_load)
-    coarse_load = send("cl", cl, cl)
+    coarse_load = send(("cl", cl, cl))
+    start_x(coarse_load)
     frame(ua, ud, 2, 0)
-    v4 = send("v4", ud, ud)
 
     interior(ud, ub, 1)
+    gone_x(coarse_load)
+    start_y(coarse_load)
+    v4 = send(("v4", ud, ud))
+    start_x(v4)
+    start_y(v4)
     interior(ub, ue, 2)
 
     arrived(coarse_mass)
@@ -298,11 +350,16 @@
     for k in range(1, INNER):
         reach = FIRST - 1 - k if k < FIRST else INNER - k
         if k == FIRST:
-            coarse_values = send("cv", cc, cc)
+            coarse_values = send(("cv", cc, cc))
+            start_x(coarse_values)
+            gone_x(coarse_values)
+            start_y(coarse_values)
             arrived(v4)
             frame(ud, ub, 1, 1)
             frame(ub, ue, 2, 0)
-            v6 = send("v6", ue, ue)
+            v6 = send(("v6", ue, ue))
+            start_x(v6)
+            start_y(v6)
             arrived(coarse_values)
         region(order[k - 1], order[k], DEEP - reach, DEEP + cy + reach, windows(COARSE_PAD, cx, reach), cl, cr)
     now = order[-1]
@@ -317,8 +374,7 @@
     lax.fori_loop(0, cy + 2, spread_row, 0)
 
     arrived(r3)
-    for copy in u2:
-        copy.wait_send()
+    gone_y(u2)
 
     def swept(y, rows, starts):
         for h in range(halves):
@@ -345,31 +401,20 @@
     swept(0, range(1, RATIO), reach3)
     swept(cy + 1, range(RATIO - 1), reach3)
 
-    def sweep_correction(src, dst, reach, base):
-        starts = windows(COL_PAD, nx, reach)
-
-        def body(i, carry):
-            y = ROW_PAD - reach + 2 * i
-            for h in range(halves):
-                for x in starts:
-                    column = [at(src, y + j, h, x) for j in range(-1, 3)]
-                    for j in range(2):
-                        total = (column[j] + column[j + 2]) + (at(src, y + j, h, x - 1) + at(src, y + j, h, x + 1))
-                        new = 0.2 * column[j + 1] + at(r, y + j, h, x) * total
-                        if base is not None:
-                            new = at(base, y + j, h, x) + new
-                        dst[y + j, h, pl.ds(x, 8), :] = new
-            return carry
-        lax.fori_loop(0, (ny + 2 * reach) // 2, body, 0)
-
-    sweep_correction(uc, ub, 2, None)
+    starts = windows(COL_PAD, nx, 2)
+
+    def second_swept(i, carry):
+        for h in range(halves):
+            for x in starts:
+                swept_twice(uc, r, None, ub, ROW_PAD - 2 + 2 * i, h, x)
+        return carry
+    lax.fori_loop(0, (ny + 4) // 2, second_swept, 0)
     arrived(v6)
-    sweep_correction(ub, ua, 1, ue)
-
-    for name, made in sent:
-        if name not in ("u0", "u2"):
-            for copy in made:
-                copy.wait_send()
+
+    for made in (r3, coarse_mass, coarse_load, v4, coarse_values, v6):
+        if made is not coarse_load and made is not coarse_values:
+            gone_x(made)
+        gone_y(made)
 
 
 def local(n_row, n_col, source_terms, initial_values, absorption):
@@ -387,13 +432,13 @@
 
     anywhere = pl.BlockSpec(memory_space=pltpu.HBM)
     inside = pl.BlockSpec(memory_space=pltpu.VMEM)
-    u, f, d = pl.pallas_call(
+    held = pl.pallas_call(
         functools.partial(kernel, sizes),
-        out_shape=(vmem(fine), vmem(fine), vmem(block)),
+        out_shape=(vmem(fine), vmem(fine), vmem(fine), vmem(block), vmem(fine)),
         in_specs=[anywhere] * 3,
-        out_specs=(inside,) * 3,
+        out_specs=(inside,) * 5,
         scratch_shapes=[
-            vmem(fine), vmem(fine), vmem(fine), vmem(fine), vmem(fine),
+            vmem(fine), vmem(fine), vmem(fine),
             vmem((cy, halves, nx, LANES)),
             vmem((cy + 2, halves, (cx + 8) * RATIO, LANES)),
             coarse, coarse, coarse, coarse, coarse,
@@ -402,7 +447,7 @@
             pltpu.SemaphoreType.DMA((count,)),
         ],
         compiler_params=pltpu.CompilerParams(
-            collective_id=0, has_side_effects=True, vmem_limit_bytes=44_000_000
+            collective_id=0, has_side_effects=True, vmem_limit_bytes=25_300_000
         ),
         name="two_grids",
     )(source_terms, initial_values, absorption)
@@ -410,12 +455,12 @@
     return pl.pallas_call(
         functools.partial(finish, (ny, nx, halves)),
         out_shape=(shape, shape),
-        in_specs=[inside] * 3,
+        in_specs=[inside] * 5,
         out_specs=(anywhere, anywhere),
-        scratch_shapes=[vmem(block), pltpu.SemaphoreType.DMA((5 * halves,))],
-        compiler_params=pltpu.CompilerParams(vmem_limit_bytes=8_000_000),
+        scratch_shapes=[vmem(fine), vmem(block), pltpu.SemaphoreType.DMA((8 * halves,))],
+        compiler_params=pltpu.CompilerParams(vmem_limit_bytes=14_000_000),
         name="finish",
-    )(u, f, d)
+    )(*held)
 
 
 def solution(mesh):

time: 64.9 us -> 72.9 us (1.12)
  Pallas kernels: 64.1 us -> 72.2 us
    pallas_call x1, Pallas kernels: 60.7 us -> 68 us  [local(): pl.pallas_call(functools.partial(kernel, sizes), out_shape=(vmem(fine), v...]
    pallas_call x1, Pallas kernels: 3.37 us -> 4.25 us  [local(): pl.pallas_call(functools.partial(finish, (ny, nx, halves)), out_shape=(sh...]
where the time goes in v4:
time: 72.9 us; the launch traced here: 72.8 us
  Pallas kernels  72.2 us (99%)
    pallas_call x1, Pallas kernels, local(): pl.pallas_call(functools.partial(kernel, sizes), out_shape=(vmem(fine), v...  68 us
    pallas_call x1, Pallas kernels, local(): pl.pallas_call(functools.partial(finish, (ny, nx, halves)), out_shape=(sh...  4.25 us

profile of v4, /device:TPU:1, one launch (start us, length us, event | category | flops | bytes accessed | tf_op | source)
XLA Modules:
  0.0 72.8 jit_solution(10769195525445308260)
XLA Ops:
  0.6 68.0 %two_grids.1 = (f32[72,2,80,128]{3,2,1,0:T(8,128)S(1)}, f32[72,2,80,128]{3,2,1,0:T(8,128)S(1)}, f32[72,2,80,128]{3,2,1,0:T(8,128)S(1)}, f32[64,2,64,128]{3,2,1,0:T(8,128)S(1)}, f32[72,2,80,128]{3,2,1,0:T(8,128)S(1)}) custom-call(f32[64,64,256]{2,1,0:T(8,128)} %f_hbm.1, f32[64,64,256]{2,1,0:T(8,128)} %u_hbm.1, f32[64,64,256]{2,1,0:T(8,128)} %a_hbm.1), custom_call_target="tpu_custom_call" | custom-call | tf_op jit(solution)/shard_map/two_grids/pallas_call | solution.py:435
  68.6 4.2 %finish.1 = (f32[64,64,256]{2,1,0:T(8,128)}, f32[64,64,256]{2,1,0:T(8,128)}) custom-call(f32[72,2,80,128]{3,2,1,0:T(8,128)S(1)} %get-tuple-element.7.e, f32[72,2,80,128]{3,2,1,0:T(8,128)S(1)} %get-tuple-element.8.v, f32[72,2,80,128]{3,2,1,0:T(8,128)S(1)} %get-tuple-element.9.f, f32[64,2,64,128]{3,2,1,0:T(8,128)S(1)} %get-tuple-element.10.d, ...), custom_call_target="tpu_custom_call" | custom-call | tf_op jit(solution)/shard_map/finish/pallas_call | solution.py:455

commit v5 on v4

--- a/solution.py
+++ b/solution.py
@@ -165,31 +165,24 @@
                 device_id=neighbour(dy, dx), device_id_type=MESH), dx == 0))
         return made
 
-    sent = []
-
     def send(*given):
-        found = [copies(*one) for one in given]
-        sent.extend(found)
-        return found
-
-    def along(made, y_only):
-        return [copy for part in made for copy, is_y in part if is_y == y_only]
-
-    def start_x(made):
-        for copy in along(made, False):
-            copy.start()
-
-    def start_y(made):
-        for copy in along(made, True):
-            copy.start()
-
-    def gone_x(made):
-        for copy in along(made, False):
-            copy.wait_send()
-
-    def gone_y(made):
-        for copy in along(made, True):
-            copy.wait_send()
+        return [copies(*one) for one in given]
+
+    def start_along(made, y_only):
+        for part in made:
+            for copy, is_y in part:
+                if is_y == y_only:
+                    copy.start()
+
+    def start(made):
+        start_along(made, False)
+        start_along(made, True)
+        return made
+
+    def gone(made):
+        for part in made:
+            for copy, _ in part:
+                copy.wait_send()
 
     def arrived(made):
         for part in made:
@@ -257,8 +250,8 @@
         copy.wait()
     for copy in f_loads:
         copy.wait()
-    start = send(("u0", ua, ua), ("f", f, f), ("r", r, r))
-    start_x(start)
+    first_halos = send(("u0", ua, ua), ("f", f, f), ("r", r, r))
+    start_along(first_halos, False)
 
     def region(src, dst, y0, y1, starts, load, rate):
         step = next(k for k in (2, 3, 1) if (y1 - y0) % k == 0)
@@ -295,25 +288,19 @@
 
     interior(ua, ub, 1)
     interior(ub, uc, 2)
-    gone_x(start)
-    start_y(start)
-    r3 = send(("r3", r, r))
-    gone_y(start)
-    start_x(r3)
-    arrived(start)
+    start_along(first_halos, True)
+    r3 = start(send(("r3", r, r)))
+    arrived(first_halos)
     frame(ua, ub, 1, 1)
     frame(ub, uc, 2, 0)
     u2 = send(("u2", uc, uc))
-    start_x(u2)
+    start_along(u2, False)
+    gone(first_halos)
 
     interior(uc, ua, 1)
     defect(1, cy - 1, own[1:-1])
-    gone_x(u2)
-    start_y(u2)
-    coarse_mass = send(("cr", cr, cr))
-    start_x(coarse_mass)
-    start_y(coarse_mass)
-    start_y(r3)
+    start_along(u2, True)
+    coarse_mass = start(send(("cr", cr, cr)))
     interior(ua, ud, 2)
     arrived(u2)
     frame(uc, ua, 1, 1)
@@ -325,15 +312,12 @@
         cl[DEEP + y, h, pl.ds(COARSE_PAD + 8 * g, 8), :] = total
     coarse_sums(sums, keep_load)
     coarse_load = send(("cl", cl, cl))
-    start_x(coarse_load)
+    start_along(coarse_load, False)
     frame(ua, ud, 2, 0)
 
     interior(ud, ub, 1)
-    gone_x(coarse_load)
-    start_y(coarse_load)
-    v4 = send(("v4", ud, ud))
-    start_x(v4)
-    start_y(v4)
+    start_along(coarse_load, True)
+    v4 = start(send(("v4", ud, ud)))
     interior(ub, ue, 2)
 
     arrived(coarse_mass)
@@ -350,16 +334,11 @@
     for k in range(1, INNER):
         reach = FIRST - 1 - k if k < FIRST else INNER - k
         if k == FIRST:
-            coarse_values = send(("cv", cc, cc))
-            start_x(coarse_values)
-            gone_x(coarse_values)
-            start_y(coarse_values)
+            coarse_values = start(send(("cv", cc, cc)))
             arrived(v4)
             frame(ud, ub, 1, 1)
             frame(ub, ue, 2, 0)
-            v6 = send(("v6", ue, ue))
-            start_x(v6)
-            start_y(v6)
+            v6 = start(send(("v6", ue, ue)))
             arrived(coarse_values)
         region(order[k - 1], order[k], DEEP - reach, DEEP + cy + reach, windows(COARSE_PAD, cx, reach), cl, cr)
     now = order[-1]
@@ -374,7 +353,7 @@
     lax.fori_loop(0, cy + 2, spread_row, 0)
 
     arrived(r3)
-    gone_y(u2)
+    gone(u2)
 
     def swept(y, rows, starts):
         for h in range(halves):
@@ -412,9 +391,7 @@
     arrived(v6)
 
     for made in (r3, coarse_mass, coarse_load, v4, coarse_values, v6):
-        if made is not coarse_load and made is not coarse_values:
-            gone_x(made)
-        gone_y(made)
+        gone(made)
 
 
 def local(n_row, n_col, source_terms, initial_values, absorption):

time: 72.9 us -> 71.2 us (0.977)
  Pallas kernels: 72.2 us -> 70.4 us
    pallas_call x1, Pallas kernels: 68 us -> 66.2 us  [local(): pl.pallas_call(functools.partial(kernel, sizes), out_shape=(vmem(fine), v...]
where the time goes in v5:
time: 71.2 us; the launch traced here: 71.1 us
  Pallas kernels  70.4 us (99%)
    pallas_call x1, Pallas kernels, local(): pl.pallas_call(functools.partial(kernel, sizes), out_shape=(vmem(fine), v...  66.2 us
    pallas_call x1, Pallas kernels, local(): pl.pallas_call(functools.partial(finish, (ny, nx, halves)), out_shape=(sh...  4.25 us

profile of v5, /device:TPU:1, one launch (start us, length us, event | category | flops | bytes accessed | tf_op | source)
XLA Modules:
  0.0 71.1 jit_solution(8158274699964876686)
XLA Ops:
  0.6 66.2 %two_grids.1 = (f32[72,2,80,128]{3,2,1,0:T(8,128)S(1)}, f32[72,2,80,128]{3,2,1,0:T(8,128)S(1)}, f32[72,2,80,128]{3,2,1,0:T(8,128)S(1)}, f32[64,2,64,128]{3,2,1,0:T(8,128)S(1)}, f32[72,2,80,128]{3,2,1,0:T(8,128)S(1)}) custom-call(f32[64,64,256]{2,1,0:T(8,128)} %f_hbm.1, f32[64,64,256]{2,1,0:T(8,128)} %u_hbm.1, f32[64,64,256]{2,1,0:T(8,128)} %a_hbm.1), custom_call_target="tpu_custom_call" | custom-call | tf_op jit(solution)/shard_map/two_grids/pallas_call | solution.py:412
  66.8 4.2 %finish.1 = (f32[64,64,256]{2,1,0:T(8,128)}, f32[64,64,256]{2,1,0:T(8,128)}) custom-call(f32[72,2,80,128]{3,2,1,0:T(8,128)S(1)} %get-tuple-element.7.e, f32[72,2,80,128]{3,2,1,0:T(8,128)S(1)} %get-tuple-element.8.v, f32[72,2,80,128]{3,2,1,0:T(8,128)S(1)} %get-tuple-element.9.f, f32[64,2,64,128]{3,2,1,0:T(8,128)S(1)} %get-tuple-element.10.d, ...), custom_call_target="tpu_custom_call" | custom-call | tf_op jit(solution)/shard_map/finish/pallas_call | solution.py:432

commit v6 on v5

--- a/solution.py
+++ b/solution.py
@@ -159,34 +159,29 @@
     def copies(name, source, landing):
         made = []
         for k, (dy, dx, src, dst) in enumerate(exchanges[name]):
-            made.append((pltpu.make_async_remote_copy(
+            made.append(pltpu.make_async_remote_copy(
                 src_ref=box(source, src), dst_ref=box(landing, dst),
                 send_sem=send_sem.at[first[name] + k], recv_sem=recv_sem.at[first[name] + k],
-                device_id=neighbour(dy, dx), device_id_type=MESH), dx == 0))
+                device_id=neighbour(dy, dx), device_id_type=MESH))
         return made
 
     def send(*given):
         return [copies(*one) for one in given]
 
-    def start_along(made, y_only):
+    def start(made):
         for part in made:
-            for copy, is_y in part:
-                if is_y == y_only:
-                    copy.start()
-
-    def start(made):
-        start_along(made, False)
-        start_along(made, True)
+            for copy in part:
+                copy.start()
         return made
 
     def gone(made):
         for part in made:
-            for copy, _ in part:
+            for copy in part:
                 copy.wait_send()
 
     def arrived(made):
         for part in made:
-            for copy, _ in part:
+            for copy in part:
                 copy.wait_recv()
 
     barrier = pltpu.get_barrier_semaphore()
@@ -205,9 +200,17 @@
             copy.start()
         return made
 
-    a_loads = loads(0, a_hbm, d, 0, 0)
-    u_loads = loads(1, u_hbm, ua, ROW_PAD, COL_PAD)
-    f_loads = loads(2, f_hbm, f, ROW_PAD, COL_PAD)
+    u_loads = loads(0, u_hbm, ua, ROW_PAD, COL_PAD)
+    f_loads = loads(1, f_hbm, f, ROW_PAD, COL_PAD)
+    a_loads = loads(2, a_hbm, d, 0, 0)
+
+    pl.semaphore_wait(barrier, len(around))
+    for copy in u_loads:
+        copy.wait()
+    first_halos = start(send(("u0", ua, ua)))
+    for copy in f_loads:
+        copy.wait()
+    first_halos += start(send(("f", f, f)))
 
     own = [COL_PAD + 8 * k for k in range(nx // 8)]
 
@@ -240,18 +243,12 @@
                 sums[y, h, pl.ds(8 * k, 8), :] = total
         return carry
     lax.fori_loop(0, cy, prepare, 0)
+    first_halos += start(send(("r", r, r)))
+    r3 = start(send(("r3", r, r)))
 
     def keep_mass(y, h, g, total):
         cr[DEEP + y, h, pl.ds(COARSE_PAD + 8 * g, 8), :] = 0.8 / (4.0 + total)
     coarse_sums(sums, keep_mass)
-
-    pl.semaphore_wait(barrier, len(around))
-    for copy in u_loads:
-        copy.wait()
-    for copy in f_loads:
-        copy.wait()
-    first_halos = send(("u0", ua, ua), ("f", f, f), ("r", r, r))
-    start_along(first_halos, False)
 
     def region(src, dst, y0, y1, starts, load, rate):
         step = next(k for k in (2, 3, 1) if (y1 - y0) % k == 0)
@@ -288,19 +285,15 @@
 
     interior(ua, ub, 1)
     interior(ub, uc, 2)
-    start_along(first_halos, True)
-    r3 = start(send(("r3", r, r)))
     arrived(first_halos)
     frame(ua, ub, 1, 1)
     frame(ub, uc, 2, 0)
-    u2 = send(("u2", uc, uc))
-    start_along(u2, False)
+    u2 = start(send(("u2", uc, uc)))
+    coarse_mass = start(send(("cr", cr, cr)))
     gone(first_halos)
 
     interior(uc, ua, 1)
     defect(1, cy - 1, own[1:-1])
-    start_along(u2, True)
-    coarse_mass = start(send(("cr", cr, cr)))
     interior(ua, ud, 2)
     arrived(u2)
     frame(uc, ua, 1, 1)
@@ -311,13 +304,11 @@
     def keep_load(y, h, g, total):
         cl[DEEP + y, h, pl.ds(COARSE_PAD + 8 * g, 8), :] = total
     coarse_sums(sums, keep_load)
-    coarse_load = send(("cl", cl, cl))
-    start_along(coarse_load, False)
+    coarse_load = start(send(("cl", cl, cl)))
     frame(ua, ud, 2, 0)
+    v4 = start(send(("v4", ud, ud)))
 
     interior(ud, ub, 1)
-    start_along(coarse_load, True)
-    v4 = start(send(("v4", ud, ud)))
     interior(ub, ue, 2)
 
     arrived(coarse_mass)

time: 71.2 us -> 64.2 us (0.902)
  Pallas kernels: 70.4 us -> 63.4 us
    pallas_call x1, Pallas kernels: 66.2 us -> 59.2 us  [local(): pl.pallas_call(functools.partial(kernel, sizes), out_shape=(vmem(fine), v...]
where the time goes in v6:
time: 64.2 us; the launch traced here: 64.1 us
  Pallas kernels  63.4 us (99%)
    pallas_call x1, Pallas kernels, local(): pl.pallas_call(functools.partial(kernel, sizes), out_shape=(vmem(fine), v...  59.2 us
    pallas_call x1, Pallas kernels, local(): pl.pallas_call(functools.partial(finish, (ny, nx, halves)), out_shape=(sh...  4.25 us

profile of v6, /device:TPU:1, one launch (start us, length us, event | category | flops | bytes accessed | tf_op | source)
XLA Modules:
  0.0 64.1 jit_solution(1423819017527427563)
XLA Ops:
  0.6 59.2 %two_grids.1 = (f32[72,2,80,128]{3,2,1,0:T(8,128)S(1)}, f32[72,2,80,128]{3,2,1,0:T(8,128)S(1)}, f32[72,2,80,128]{3,2,1,0:T(8,128)S(1)}, f32[64,2,64,128]{3,2,1,0:T(8,128)S(1)}, f32[72,2,80,128]{3,2,1,0:T(8,128)S(1)}) custom-call(f32[64,64,256]{2,1,0:T(8,128)} %f_hbm.1, f32[64,64,256]{2,1,0:T(8,128)} %u_hbm.1, f32[64,64,256]{2,1,0:T(8,128)} %a_hbm.1), custom_call_target="tpu_custom_call" | custom-call | tf_op jit(solution)/shard_map/two_grids/pallas_call | solution.py:403
  59.8 4.2 %finish.1 = (f32[64,64,256]{2,1,0:T(8,128)}, f32[64,64,256]{2,1,0:T(8,128)}) custom-call(f32[72,2,80,128]{3,2,1,0:T(8,128)S(1)} %get-tuple-element.7.e, f32[72,2,80,128]{3,2,1,0:T(8,128)S(1)} %get-tuple-element.8.v, f32[72,2,80,128]{3,2,1,0:T(8,128)S(1)} %get-tuple-element.9.f, f32[64,2,64,128]{3,2,1,0:T(8,128)S(1)} %get-tuple-element.10.d, ...), custom_call_target="tpu_custom_call" | custom-call | tf_op jit(solution)/shard_map/finish/pallas_call | solution.py:423

commit v7 on v6

--- a/solution.py
+++ b/solution.py
@@ -88,6 +88,16 @@
     return [min(x, high - 8) for x in range(low, high, 8)]
 
 
+def loop(low, high, times, one):
+    times = times if (high - low) % times == 0 else 1
+
+    def body(i, carry):
+        for t in range(times):
+            one(low + i * times + t)
+        return carry
+    lax.fori_loop(0, (high - low) // times, body, 0)
+
+
 def swept_twice(src, r, base, dst, y, h, x):
     column = [src[y + j, h, pl.ds(x, 8), :] for j in range(-1, 3)]
     for j in range(2):
@@ -218,14 +228,13 @@
         return ref[y, h, pl.ds(x, 8), :]
 
     def coarse_sums(ref, done):
-        def body(y, carry):
+        def one(y):
             for h in range(halves):
                 for g in range(cx // 8):
                     parts = [sums[y, h, pl.ds(32 * g + k, 8, stride=4), :] for k in range(4)]
                     total = ((parts[0] + parts[1]) + (parts[2] + parts[3])) * 0.25
                     done(y, h, g, total)
-            return carry
-        lax.fori_loop(0, cy, body, 0)
+        loop(0, cy, 4, one)
 
     for copy in a_loads:
         copy.wait()
@@ -251,7 +260,7 @@
     coarse_sums(sums, keep_mass)
 
     def region(src, dst, y0, y1, starts, load, rate):
-        step = next(k for k in (2, 3, 1) if (y1 - y0) % k == 0)
+        step = next(k for k in (8, 6, 4, 3, 2, 1) if (y1 - y0) % k == 0 and k * len(starts) <= 18)
 
         def body(i, carry):
             y = y0 + step * i
@@ -275,13 +284,12 @@
         region(src, dst, ROW_PAD, ROW_PAD + ny, [full[0], full[-1]], f, r)
 
     def defect(y0, y1, starts):
-        def body(y, carry):
+        def one(y):
             for h in range(halves):
                 for x in starts:
                     a, b, c, e = left_over(ua, f, d, ROW_PAD + RATIO * y, h, x)
                     sums[y, h, pl.ds(x - COL_PAD, 8), :] = (a + b) + (c + e)
-            return carry
-        lax.fori_loop(y0, y1, body, 0)
+        loop(y0, y1, 2 if len(starts) <= 2 else 1, one)
 
     interior(ua, ub, 1)
     interior(ub, uc, 2)
@@ -314,12 +322,11 @@
     arrived(coarse_mass)
     arrived(coarse_load)
 
-    def first_coarse(y, carry):
+    def first_coarse(y):
         for h in range(halves):
             for x in windows(COARSE_PAD, cx, DEEP - 1):
                 ca[y, h, pl.ds(x, 8), :] = at(cr, y, h, x) * at(cl, y, h, x)
-        return carry
-    lax.fori_loop(1, cy + 2 * DEEP - 1, first_coarse, 0)
+    loop(1, cy + 2 * DEEP - 1, 4, first_coarse)
 
     order = [ca, cb, ca, cb, cc, ca, cb, ca, cb]
     for k in range(1, INNER):
@@ -334,14 +341,13 @@
         region(order[k - 1], order[k], DEEP - reach, DEEP + cy + reach, windows(COARSE_PAD, cx, reach), cl, cr)
     now = order[-1]
 
-    def spread_row(y, carry):
+    def spread_row(y):
         for h in range(halves):
             for w in range((cx + 2 + 7) // 8):
                 c = at(now, DEEP - 1 + y, h, COARSE_PAD - 1 + 8 * w)
                 for k in range(RATIO):
                     spread[y, h, pl.ds(32 * w + k, 8, stride=4), :] = c
-        return carry
-    lax.fori_loop(0, cy + 2, spread_row, 0)
+    loop(0, cy + 2, 3, spread_row)
 
     arrived(r3)
     gone(u2)

time: 64.2 us -> 63.6 us (level)
  no operation moved by 1% of the time
where the time goes in v7:
time: 63.6 us; the launch traced here: 63.5 us
  Pallas kernels  62.8 us (99%)
  between operations  0.64 us (1%)
    pallas_call x1, Pallas kernels, local(): pl.pallas_call(functools.partial(kernel, sizes), out_shape=(vmem(fine), v...  58.6 us
    pallas_call x1, Pallas kernels, local(): pl.pallas_call(functools.partial(finish, (ny, nx, halves)), out_shape=(sh...  4.25 us

profile of v7, /device:TPU:1, one launch (start us, length us, event | category | flops | bytes accessed | tf_op | source)
XLA Modules:
  0.0 63.5 jit_solution(14237523779684853494)
XLA Ops:
  0.6 58.6 %two_grids.1 = (f32[72,2,80,128]{3,2,1,0:T(8,128)S(1)}, f32[72,2,80,128]{3,2,1,0:T(8,128)S(1)}, f32[72,2,80,128]{3,2,1,0:T(8,128)S(1)}, f32[64,2,64,128]{3,2,1,0:T(8,128)S(1)}, f32[72,2,80,128]{3,2,1,0:T(8,128)S(1)}) custom-call(f32[64,64,256]{2,1,0:T(8,128)} %f_hbm.1, f32[64,64,256]{2,1,0:T(8,128)} %u_hbm.1, f32[64,64,256]{2,1,0:T(8,128)} %a_hbm.1), custom_call_target="tpu_custom_call" | custom-call | tf_op jit(solution)/shard_map/two_grids/pallas_call | solution.py:409
  59.2 4.2 %finish.1 = (f32[64,64,256]{2,1,0:T(8,128)}, f32[64,64,256]{2,1,0:T(8,128)}) custom-call(f32[72,2,80,128]{3,2,1,0:T(8,128)S(1)} %get-tuple-element.7.e, f32[72,2,80,128]{3,2,1,0:T(8,128)S(1)} %get-tuple-element.8.v, f32[72,2,80,128]{3,2,1,0:T(8,128)S(1)} %get-tuple-element.9.f, f32[64,2,64,128]{3,2,1,0:T(8,128)S(1)} %get-tuple-element.10.d, ...), custom_call_target="tpu_custom_call" | custom-call | tf_op jit(solution)/shard_map/finish/pallas_call | solution.py:429

commit v8 on v7

--- a/solution.py
+++ b/solution.py
@@ -50,19 +50,19 @@
 def plan(ny, nx):
     rows, cols = (ROW_PAD, ny), (COL_PAD, nx)
     crows, ccols = (DEEP, ny // RATIO), (COARSE_PAD, nx // RATIO)
-    coarse = edge_rects(crows, ccols, 0, DEEP - 1)
-    coarse = coarse + corner_rects(crows, ccols, 0, 2, 4) + corner_rects(crows, ccols, 2, 4, 2)
-    values = edge_rects(crows, ccols, 0, DEEP)
-    values = values + corner_rects(crows, ccols, 0, 3, 5) + corner_rects(crows, ccols, 3, 5, 2)
+    coarse = corner_rects(crows, ccols, 0, 2, 4) + corner_rects(crows, ccols, 2, 4, 2)
+    coarse = coarse + edge_rects(crows, ccols, 0, DEEP - 1)
+    values = corner_rects(crows, ccols, 0, 3, 5) + corner_rects(crows, ccols, 3, 5, 2)
+    values = values + edge_rects(crows, ccols, 0, DEEP)
     exchanges = {
-        "u0": edge_rects(rows, cols, 0, 2) + corner_rects(rows, cols, 0, 1, 1),
+        "u0": corner_rects(rows, cols, 0, 1, 1) + edge_rects(rows, cols, 0, 2),
         "f": edge_rects(rows, cols, 0, 1),
         "r": edge_rects(rows, cols, 0, 1),
         "r3": edge_rects(rows, cols, 1, 3) + corner_rects(rows, cols, 0, 2, 2),
-        "u2": edge_rects(rows, cols, 0, 2) + corner_rects(rows, cols, 0, 1, 1),
+        "u2": corner_rects(rows, cols, 0, 1, 1) + edge_rects(rows, cols, 0, 2),
         "cr": coarse,
         "cl": coarse,
-        "v4": edge_rects(rows, cols, 0, 2) + corner_rects(rows, cols, 0, 1, 1),
+        "v4": corner_rects(rows, cols, 0, 1, 1) + edge_rects(rows, cols, 0, 2),
         "v6": edge_rects(rows, cols, 0, 1),
         "cv": values,
     }

time: 63.6 us -> 63.8 us (level)
  no operation moved by 1% of the time
where the time goes in v8:
time: 63.8 us; the launch traced here: 63.7 us
  Pallas kernels  63.1 us (99%)
  between operations  0.64 us (1%)
    pallas_call x1, Pallas kernels, local(): pl.pallas_call(functools.partial(kernel, sizes), out_shape=(vmem(fine), v...  58.8 us
    pallas_call x1, Pallas kernels, local(): pl.pallas_call(functools.partial(finish, (ny, nx, halves)), out_shape=(sh...  4.25 us

profile of v8, /device:TPU:1, one launch (start us, length us, event | category | flops | bytes accessed | tf_op | source)
XLA Modules:
  0.0 63.7 jit_solution(3928348573353532283)
XLA Ops:
  0.6 58.8 %two_grids.1 = (f32[72,2,80,128]{3,2,1,0:T(8,128)S(1)}, f32[72,2,80,128]{3,2,1,0:T(8,128)S(1)}, f32[72,2,80,128]{3,2,1,0:T(8,128)S(1)}, f32[64,2,64,128]{3,2,1,0:T(8,128)S(1)}, f32[72,2,80,128]{3,2,1,0:T(8,128)S(1)}) custom-call(f32[64,64,256]{2,1,0:T(8,128)} %f_hbm.1, f32[64,64,256]{2,1,0:T(8,128)} %u_hbm.1, f32[64,64,256]{2,1,0:T(8,128)} %a_hbm.1), custom_call_target="tpu_custom_call" | custom-call | tf_op jit(solution)/shard_map/two_grids/pallas_call | solution.py:409
  59.5 4.2 %finish.1 = (f32[64,64,256]{2,1,0:T(8,128)}, f32[64,64,256]{2,1,0:T(8,128)}) custom-call(f32[72,2,80,128]{3,2,1,0:T(8,128)S(1)} %get-tuple-element.7.e, f32[72,2,80,128]{3,2,1,0:T(8,128)S(1)} %get-tuple-element.8.v, f32[72,2,80,128]{3,2,1,0:T(8,128)S(1)} %get-tuple-element.9.f, f32[64,2,64,128]{3,2,1,0:T(8,128)S(1)} %get-tuple-element.10.d, ...), custom_call_target="tpu_custom_call" | custom-call | tf_op jit(solution)/shard_map/finish/pallas_call | solution.py:429
